TPU v7x, 32 devices: a whole 2x2x4 slice. The times are simulated.
32 devices in a mesh: group: 8 (over y, x, core), pos: 4 (over z).
Axes of the slice: x: 2, y: 2, z: 4, core: 2. Of those that a mesh axis runs over, the one named last changes fastest.
Arguments:
- features: bfloat16 [384, 256, 256], P(('group', 'pos')), may hold values from -6 to 6
- gain_attn: float32 [256], replicated, may hold values from 0.1 to 1.9
- w_query: bfloat16 [256, 256], replicated, as said below
- w_key: bfloat16 [256, 256], replicated, as said below
- w_value: bfloat16 [256, 256], replicated, may hold values from -0.375 to 0.375
- w_out: bfloat16 [256, 256], replicated, may hold values from -0.375 to 0.375
- gain_ffn: float32 [256], replicated, may hold values from 0.1 to 1.9
- w_up: bfloat16 [256, 1024], replicated, may hold values from -0.375 to 0.375
- w_down: bfloat16 [1024, 256], replicated, may hold values from -0.1875 to 0.1875
- counts: int32 [6], replicated, may hold values from 4 to 64, as said below
- offsets: int32 [6], replicated, may hold values from 0 to 380, as said below
Outputs:
- result: bfloat16 [384, 256, 256], P(('group', 'pos'))
Inputs may be any that keep to these rules, and one draw needn't show every extreme that they name: `counts`: each mixture has 4 to 64 groups, and one mixture has exactly 64. Mixture m occupies slots offsets[m] to offsets[m] + counts[m] - 1; the mixtures follow one another in order without intersection. `w_query`: a dense matrix of independent entries. `w_key`: a dense matrix of independent entries.
All inputs are finite; a program needn't handle non-finite values.
Results may differ from a plain program's by a relative error of at most 0.0065.
Values may be sent and summed in bfloat16 or wider, within the bound.
No kernel may reach another device: no remote copies, remote signals or barrier semaphores. Data moves between devices by JAX's collectives and lax.ppermute only.
A program may use at most 192 MiB of HBM per device.

v0:
```python
import math
import jax
import jax.numpy as jnp
from jax import lax
from jax.sharding import PartitionSpec as P

HEADS = 8
epsilon = 1e-05
masked_value = -1e30


def segment_ids(counts, offsets, slots_total):
    slots = jnp.arange(slots_total, dtype=jnp.int32)[:, None]
    inside = (slots >= offsets[None, :]) & (slots < offsets[None, :] + counts[None, :])
    labels = jnp.arange(counts.shape[0], dtype=jnp.int32)[None, :] + 1
    return jnp.sum(jnp.where(inside, labels, 0), axis=1) - 1


def layer_norm(values, gain):
    floats = values.astype(jnp.float32)
    average = jnp.mean(floats, axis=-1, keepdims=True)
    centred = floats - average
    spread = jnp.mean(centred * centred, axis=-1, keepdims=True)
    return (centred * lax.rsqrt(spread + epsilon) * gain).astype(jnp.bfloat16)


def feed_forward(middle, gain_ffn, w_up, w_down):
    second = layer_norm(middle, gain_ffn)
    hidden = jnp.maximum(jnp.dot(second, w_up, preferred_element_type=jnp.float32), 0.0).astype(
        jnp.bfloat16
    )
    return (
        middle.astype(jnp.float32) + jnp.dot(hidden, w_down, preferred_element_type=jnp.float32)
    ).astype(jnp.bfloat16)


def local(
    features, gain_attn, w_query, w_key, w_value, w_out, gain_ffn, w_up, w_down, counts, offsets
):
    group_devices = lax.axis_size("group")
    pos_devices = lax.axis_size("pos")
    local_groups = features.shape[0]
    width = features.shape[2]
    slots_total = local_groups * group_devices * pos_devices
    head_dim = width // HEADS
    scale = 1.0 / math.sqrt(head_dim)
    gathered = lax.all_to_all(features, ("group", "pos"), split_axis=1, concat_axis=0, tiled=True)
    owned = gathered.shape[1]
    labels = segment_ids(counts, offsets, slots_total)
    flat = gathered.reshape(slots_total * owned, width)
    normed = layer_norm(flat, gain_attn)

    def project(weight):
        product = jnp.dot(normed, weight, preferred_element_type=jnp.float32).astype(jnp.bfloat16)
        return product.reshape(slots_total, owned, HEADS, head_dim)

    query = project(w_query)
    keys = project(w_key)
    values = project(w_value)
    block = min(512, slots_total)

    def attend(start):
        block_query = lax.dynamic_slice_in_dim(query, start, block, 0)
        block_labels = lax.dynamic_slice_in_dim(labels, start, block, 0)
        scores = (
            jnp.einsum("qphe,kphe->phqk", block_query, keys, preferred_element_type=jnp.float32)
            * scale
        )
        allowed = (block_labels[:, None] == labels[None, :]) & (block_labels[:, None] >= 0)
        scores = jnp.where(allowed[None, None], scores, masked_value)
        highest = jnp.max(scores, axis=-1, keepdims=True)
        exponent = jnp.exp(scores - highest)
        total = jnp.sum(exponent, axis=-1, keepdims=True)
        weights = (exponent / total).astype(jnp.bfloat16)
        context = jnp.einsum(
            "phqk,kphe->qphe", weights, values, preferred_element_type=jnp.float32
        ).astype(jnp.bfloat16)
        return jnp.where((block_labels >= 0)[:, None, None, None], context, jnp.zeros_like(context))

    starts = jnp.arange(slots_total // block, dtype=jnp.int32) * block
    context = lax.map(attend, starts).reshape(slots_total * owned, width)
    middle = (
        flat.astype(jnp.float32) + jnp.dot(context, w_out, preferred_element_type=jnp.float32)
    ).astype(jnp.bfloat16)
    middle = middle.reshape(slots_total, owned, width)
    returned = lax.all_to_all(middle, ("group", "pos"), split_axis=0, concat_axis=1, tiled=True)
    finished = feed_forward(returned.reshape(-1, width), gain_ffn, w_up, w_down)
    return finished.reshape(returned.shape)


def solution(mesh):
    return jax.shard_map(
        local,
        mesh=mesh,
        in_specs=(
            P(("group", "pos"), None, None),
            P(),
            P(),
            P(),
            P(),
            P(),
            P(),
            P(),
            P(),
            P(),
            P(),
        ),
        out_specs=P(("group", "pos"), None, None),
        check_vma=False,
    )
```

profile of v0, /device:TPU:1, one launch (start us, length us, event | category | flops | bytes accessed | tf_op | source)
XLA Modules:
  0.0 253.2 jit_solution(11873321647180178728)
XLA Ops:
  0.0 0.0 copy-start
  0.0 0.0 copy-start.9
  0.0 0.0 copy-start.7
  0.0 3.7 %copy.33 = bf16[12,256,256]{2,0,1:T(8,128)(2,1)} copy(bf16[12,256,256]{2,1,0:T(8,128)(2,1)} %param.11) | data formatting | bytes 3145728 | tf_op args[0]
  3.8 7.1 %all-to-all-start = ((bf16[12,256,256]{2,0,1:T(8,128)(2,1)}), bf16[12,256,256]{2,0,1:T(8,128)(2,1)S(1)}, u32[]{:S(2)}, u32[]{:S(2)}) async-start(bf16[12,256,256]{2,0,1:T(8,128)(2,1)} %copy.33), calls=%async_computation | async-start | bytes 4194304 | tf_op jit(solution)/shard_map/all_to_all | solution.py:47
  10.8 0.0 copy-done.9
  10.9 0.0 copy-done.7
  10.9 0.1 select_reduce_fusion
  11.0 0.2 compare_and_fusion
  11.2 48.0 %all-to-all-done = bf16[12,256,256]{2,0,1:T(8,128)(2,1)S(1)} async-done(((bf16[12,256,256]{2,0,1:T(8,128)(2,1)}), bf16[12,256,256]{2,0,1:T(8,128)(2,1)S(1)}, u32[]{:S(2)}, u32[]{:S(2)}) %all-to-all-start) | async-done | bytes 1572896 | tf_op jit(solution)/shard_map/all_to_all | solution.py:47
  59.2 2.2 bitcast_reduce_fusion.1
  61.4 0.0 copy-start.5
  61.4 0.1 div.29
  61.5 2.8 %fusion.21 = f32[32,12,8]{2,1,0:T(8,128)S(1)} fusion(f32[12,32,8,256]{3,2,0,1:T(8,128)} %get-tuple-element.16, f32[32,12,8]{2,1,0:T(8,128)S(1)} %broadcast_multiply_fusion), kind=kLoop, calls=%fused_computation.36 | loop fusion | flops 2356224 | bytes 3170304 | tf_op jit(solution)/shard_map/reduce_sum | solution.py:23
  64.3 0.0 copy-start.1
  64.4 0.1 rsqrt.23
  64.5 0.0 copy-done.5
  64.5 3.1 %fusion.19 = bf16[3072,256]{1,0:T(8,128)(2,1)S(1)} fusion(f32[12,32,8,256]{3,2,0,1:T(8,128)} %get-tuple-element.16, f32[256]{0:T(256)S(1)} %copy-done.5, f32[3072]{0:T(1024)S(1)} %rsqrt.23, f32[3072]{0:T(1024)S(1)} %div.29), kind=kLoop, calls=%fused_computation.32 | loop fusion | flops 3145728 | bytes 4744192 | tf_op jit(solution)/shard_map/convert_element_type | solution.py:24
  67.6 0.0 copy-done.1
  67.6 1.7 convolution_convert_fusion.1
  69.4 0.0 copy-start.2
  69.4 7.9 %reshape.166 = bf16[384,8,8,32]{3,2,1,0:T(8,128)(2,1)} reshape(bf16[3072,256]{1,0:T(8,128)(2,1)} %convolution_convert_fusion.1) | data formatting | bytes 3145728 | tf_op jit(solution)/shard_map/reshape | solution.py:55
  77.2 0.0 copy-done.2
  77.2 1.7 convolution_convert_fusion
  78.9 7.9 %reshape.167 = bf16[384,8,8,32]{3,2,1,0:T(8,128)(2,1)} reshape(bf16[3072,256]{1,0:T(8,128)(2,1)} %convolution_convert_fusion) | data formatting | bytes 3145728 | tf_op jit(solution)/shard_map/reshape | solution.py:55
  86.8 0.0 copy-done.3
  86.8 1.7 convolution_convert_fusion.2
  88.5 7.9 %reshape.165 = bf16[384,8,8,32]{3,2,1,0:T(8,128)(2,1)} reshape(bf16[3072,256]{1,0:T(8,128)(2,1)} %convolution_convert_fusion.2) | data formatting | bytes 3145728 | tf_op jit(solution)/shard_map/reshape | solution.py:55
  96.4 22.9 %fusion.7 = f32[8,8,384,384]{2,3,1,0:T(8,128)} fusion(bf16[384,8,8,32]{3,2,1,0:T(8,128)(2,1)} %reshape.167, bf16[384,8,8,32]{3,2,1,0:T(8,128)(2,1)} %reshape.166), kind=kOutput, calls=%fused_computation.11 | convolution fusion | flops 603979776 | bytes 40894464 | tf_op jit(solution)/shard_map/while/body/eval_jaxpr/qphe,kphe->phqk/dot_general | solution.py:66
  119.3 42.9 %fusion.32 = (f32[8,8,384]{2,1,0:T(8,128)S(1)}, f32[8,8,384,384]{2,3,1,0:T(8,128)}) fusion(f32[8,8,384,384]{2,3,1,0:T(8,128)} %fusion.7, pred[384,384]{0,1:T(8,128)(4,1)S(1)} %compare_and_fusion), kind=kOutput, calls=%fused_computation.55 | output fusion | flops 56623488 | bytes 75743232 | tf_op jit(solution)/shard_map/while/body/eval_jaxpr/sub | solution.py:72
  162.3 17.4 %select_bitcast_fusion = bf16[384,8,8,32]{0,3,2,1:T(8,128)(2,1)S(1)} fusion(pred[384]{0:T(512)(128)(4,1)S(1)} %broadcast_compare_fusion, f32[8,8,384,384]{2,3,1,0:T(8,128)} %get-tuple-element.24, f32[8,8,384]{2,1,0:T(8,128)S(1)} %get-tuple-element.17, bf16[384,8,8,32]{3,2,1,0:T(8,128)(2,1)} %reshape.165), kind=kOutput, calls=%fused_computation.38 | convolution fusion | flops 624427008 | bytes 40993152 | tf_op jit(solution)/shard_map/while/body/eval_jaxpr/phqk,kphe->qphe/dot_general | solution.py:75
  179.7 9.3 %copy.39 = bf16[384,8,8,32]{3,2,1,0:T(8,128)(2,1)} copy(bf16[384,8,8,32]{0,3,2,1:T(8,128)(2,1)S(1)} %select_bitcast_fusion) | data formatting | bytes 3145728 | tf_op jit(solution)/shard_map/while/body/eval_jaxpr/jit(_where)/select_n | solution.py:78
  189.0 7.5 %reshape.168 = bf16[3072,256]{1,0:T(8,128)(2,1)S(1)} reshape(bf16[384,8,8,32]{3,2,1,0:T(8,128)(2,1)} %copy.39) | data formatting | bytes 3145728 | tf_op jit(solution)/shard_map/reshape | solution.py:81
  196.5 0.0 copy-done.4
  196.6 2.5 fusion.25
  199.0 40.7 %all_to_all.8 = bf16[384,8,256]{2,1,0:T(8,128)(2,1)S(1)} all-to-all(bf16[384,8,256]{2,1,0:T(8,128)(2,1)S(1)} %fusion.25), channel_id=1, replica_groups=mesh['group'=8,'pos'=4] {'group','pos'}, dimensions={0} | all-to-all | bytes 3145728 | tf_op jit(solution)/shard_map/all_to_all | solution.py:86
  239.7 0.5 bitcast_reduce_fusion
  240.2 0.0 copy-start.6
  240.2 2.0 copy.40
  242.2 0.9 fusion.16
  243.2 0.0 copy-start.8
  243.2 0.1 div.34
  243.4 0.1 rsqrt.25
  243.5 0.0 copy-done.6
  243.5 3.1 %fusion.14 = bf16[3072,256]{1,0:T(8,128)(2,1)S(1)} fusion(f32[32,12,8,256]{3,2,0,1:T(8,128)} %copy.40, f32[256]{0:T(256)S(1)} %copy-done.6, f32[3072]{0:T(1024)S(1)} %rsqrt.25, f32[3072]{0:T(1024)S(1)} %div.34), kind=kLoop, calls=%fused_computation.24 | loop fusion | flops 3145728 | bytes 4744192 | tf_op jit(solution)/shard_map/convert_element_type | solution.py:24
  246.6 0.0 copy-done
  246.6 0.0 copy-done.8
  246.6 6.6 %fusion.10 = bf16[3072,256]{1,0:T(8,128)(2,1)} fusion(f32[3072,256]{1,0:T(8,128)} %bitcast.58, bf16[1024,256]{1,0:T(8,128)(2,1)S(1)} %copy-done, bf16[3072,256]{1,0:T(8,128)(2,1)S(1)} %fusion.14, bf16[256,1024]{1,0:T(8,128)(2,1)S(1)} %copy-done.8), kind=kOutput, calls=%fused_computation.16 | convolution fusion | flops 3229089792 | bytes 7340032 | tf_op jit(solution)/shard_map/dot_general | solution.py:33
  (10 shorter events, 0.1 us)
Async XLA Ops:
  0.0 246.6 %copy-start = (bf16[1024,256]{1,0:T(8,128)(2,1)S(1)}, bf16[1024,256]{1,0:T(8,128)(2,1)}, u32[]{:S(2)}) copy-start(bf16[1024,256]{1,0:T(8,128)(2,1)} %param.19) | copy-start | bytes 1572868
  0.0 10.8 %copy-start.9 = (s32[6]{0:T(128)S(1)}, s32[6]{0:T(128)}, u32[]{:S(2)}) copy-start(s32[6]{0:T(128)} %param.20) | copy-start | bytes 76
  0.0 10.9 %copy-start.7 = (s32[6]{0:T(128)S(1)}, s32[6]{0:T(128)}, u32[]{:S(2)}) copy-start(s32[6]{0:T(128)} %param.21) | copy-start | bytes 76
  3.8 55.4 %all-to-all-start = ((bf16[12,256,256]{2,0,1:T(8,128)(2,1)}), bf16[12,256,256]{2,0,1:T(8,128)(2,1)S(1)}, u32[]{:S(2)}, u32[]{:S(2)}) async-start(bf16[12,256,256]{2,0,1:T(8,128)(2,1)} %copy.33), calls=%async_computation | async-start | bytes 4194304 | tf_op jit(solution)/shard_map/all_to_all | solution.py:47
  61.4 3.1 %copy-start.5 = (f32[256]{0:T(256)S(1)}, f32[256]{0:T(256)}, u32[]{:S(2)}) copy-start(f32[256]{0:T(256)} %param.12) | copy-start | bytes 3076
  64.3 3.3 %copy-start.1 = (bf16[256,256]{1,0:T(8,128)(2,1)S(1)}, bf16[256,256]{1,0:T(8,128)(2,1)}, u32[]{:S(2)}) copy-start(bf16[256,256]{1,0:T(8,128)(2,1)} %param.13) | copy-start | bytes 393220
  69.4 7.9 %copy-start.2 = (bf16[256,256]{1,0:T(8,128)(2,1)S(1)}, bf16[256,256]{1,0:T(8,128)(2,1)}, u32[]{:S(2)}) copy-start(bf16[256,256]{1,0:T(8,128)(2,1)} %param.14) | copy-start | bytes 393220
  78.9 7.9 %copy-start.3 = (bf16[256,256]{1,0:T(8,128)(2,1)S(1)}, bf16[256,256]{1,0:T(8,128)(2,1)}, u32[]{:S(2)}) copy-start(bf16[256,256]{1,0:T(8,128)(2,1)} %param.15) | copy-start | bytes 393220
  189.0 7.6 %copy-start.4 = (bf16[256,256]{1,0:T(8,128)(2,1)S(1)}, bf16[256,256]{1,0:T(8,128)(2,1)}, u32[]{:S(2)}) copy-start(bf16[256,256]{1,0:T(8,128)(2,1)} %param.16) | copy-start | bytes 393220
  240.2 3.3 %copy-start.6 = (f32[256]{0:T(256)S(1)}, f32[256]{0:T(256)}, u32[]{:S(2)}) copy-start(f32[256]{0:T(256)} %param.17) | copy-start | bytes 3076
  243.2 3.4 %copy-start.8 = (bf16[256,1024]{1,0:T(8,128)(2,1)S(1)}, bf16[256,1024]{1,0:T(8,128)(2,1)}, u32[]{:S(2)}) copy-start(bf16[256,1024]{1,0:T(8,128)(2,1)} %param.18) | copy-start | bytes 1572868
where the time goes:
time: 254 us; the launch traced here: 253 us
  other arithmetic  55.9 us (22%)
  matrix products  54.6 us (21%)
  waiting for transfers between devices  48 us (19%)
  local copies, waits for them, and re-layouts  46.7 us (18%)
  blocking collectives  40.7 us (16%)
  starting transfers between devices  7.08 us (3%)
    all_to_all x1, waiting for transfers between devices, local(): lax.all_to_all(features, ('group', 'pos'), split_axis=1, concat_axis=0, t...  48 us
    sub x1, other arithmetic, attend(): exponent = jnp.exp(scores - highest)  42.9 us
    all_to_all x1, blocking collectives, local(): lax.all_to_all(middle, ('group', 'pos'), split_axis=0, concat_axis=1, til...  40.7 us
    reshape x3, local copies, waits for them, and re-layouts, project(): return product.reshape(slots_total, owned, HEADS, head_dim)  23.6 us
    dot_general x1, matrix products, attend(): jnp.einsum('qphe,kphe->phqk', block_query, keys, preferred_element_type=j...  22.9 us
    dot_general x1, matrix products, attend(): jnp.einsum('phqk,kphe->qphe', weights, values, preferred_element_type=jnp...  17.4 us
    select_n x1, local copies, waits for them, and re-layouts, attend(): jnp.where((block_labels >= 0)[:, None, None, None], context, jnp.zeros_li...  9.28 us
    reshape x1, local copies, waits for them, and re-layouts, local(): context = lax.map(attend, starts).reshape(slots_total * owned, width)  7.55 us
  transfers between devices with their start and end apart: 1, of which 1 were waited for; matrix products, arithmetic and copies ran while one was open for 0% of the time, Pallas kernels for 0%

commit v1 on v0

--- a/solution.py
+++ b/solution.py
@@ -44,7 +44,15 @@
     slots_total = local_groups * group_devices * pos_devices
     head_dim = width // HEADS
     scale = 1.0 / math.sqrt(head_dim)
-    gathered = lax.all_to_all(features, ("group", "pos"), split_axis=1, concat_axis=0, tiled=True)
+    gathered = jnp.concatenate(
+        lax.all_to_all(
+            jnp.stack(jnp.split(features, lax.axis_size(("group", "pos")), axis=1)),
+            ("group", "pos"),
+            0,
+            0,
+        ),
+        axis=0,
+    )
     owned = gathered.shape[1]
     labels = segment_ids(counts, offsets, slots_total)
     flat = gathered.reshape(slots_total * owned, width)

time: 254 us -> 288 us (1.13)
  local copies, waits for them, and re-layouts: 46.7 us -> 91.2 us
  waiting for transfers between devices: 48 us -> 37.1 us
  other arithmetic: 55.9 us -> 50.9 us
  matrix products: 54.6 us -> 58 us
    unnamed x21 -> x53, local copies, waits for them, and re-layouts: 3.79 us -> 45.3 us
    all_to_all x1, waiting for transfers between devices: 48 us -> 37.1 us  [local(): lax.all_to_all(jnp.stack(jnp.split(features, lax.axis_size(('group', 'pos...]
where the time goes in v1:
time: 288 us; the launch traced here: 285 us
  local copies, waits for them, and re-layouts  91.2 us (32%)
  matrix products  58 us (20%)
  other arithmetic  50.9 us (18%)
  blocking collectives  40.7 us (14%)
  waiting for transfers between devices  37.1 us (13%)
  starting transfers between devices  7.08 us (2%)
    unnamed x53, local copies, waits for them, and re-layouts  45.3 us
    sub x1, other arithmetic, attend(): exponent = jnp.exp(scores - highest)  42.9 us
    all_to_all x1, blocking collectives, local(): lax.all_to_all(middle, ('group', 'pos'), split_axis=0, concat_axis=1, til...  40.7 us
    all_to_all x1, waiting for transfers between devices, local(): lax.all_to_all(jnp.stack(jnp.split(features, lax.axis_size(('group', 'pos...  37.1 us
    reshape x3, local copies, waits for them, and re-layouts, project(): return product.reshape(slots_total, owned, HEADS, head_dim)  23.6 us
    dot_general x1, matrix products, attend(): jnp.einsum('qphe,kphe->phqk', block_query, keys, preferred_element_type=j...  22.9 us
    dot_general x1, matrix products, attend(): jnp.einsum('phqk,kphe->qphe', weights, values, preferred_element_type=jnp...  18.5 us
    select_n x1, local copies, waits for them, and re-layouts, attend(): jnp.where((block_labels >= 0)[:, None, None, None], context, jnp.zeros_li...  9.94 us
  transfers between devices with their start and end apart: 1, of which 1 were waited for; matrix products, arithmetic and copies ran while one was open for 0% of the time, Pallas kernels for 0%

profile of v1, /device:TPU:1, one launch (start us, length us, event | category | flops | bytes accessed | tf_op | source)
XLA Modules:
  0.0 285.2 jit_solution(11395651524798161817)
XLA Ops:
  0.0 1.5 constant_dynamic-update-slice_fusion.31
  1.5 1.4 constant_dynamic-update-slice_fusion.30
  2.9 1.4 constant_dynamic-update-slice_fusion.29
  4.3 1.4 constant_dynamic-update-slice_fusion.28
  5.7 1.4 constant_dynamic-update-slice_fusion.27
  7.2 1.4 constant_dynamic-update-slice_fusion.26
  8.6 1.4 constant_dynamic-update-slice_fusion.25
  10.0 1.4 constant_dynamic-update-slice_fusion.24
  11.4 1.4 constant_dynamic-update-slice_fusion.23
  12.9 1.4 constant_dynamic-update-slice_fusion.22
  14.3 1.4 constant_dynamic-update-slice_fusion.21
  15.7 1.4 constant_dynamic-update-slice_fusion.20
  17.1 1.4 constant_dynamic-update-slice_fusion.19
  18.5 1.4 constant_dynamic-update-slice_fusion.18
  20.0 1.4 constant_dynamic-update-slice_fusion.17
  21.4 1.4 constant_dynamic-update-slice_fusion.16
  22.8 1.4 constant_dynamic-update-slice_fusion.15
  24.2 1.4 constant_dynamic-update-slice_fusion.14
  25.6 1.4 constant_dynamic-update-slice_fusion.13
  27.1 1.4 constant_dynamic-update-slice_fusion.12
  28.5 1.4 constant_dynamic-update-slice_fusion.11
  29.9 1.4 constant_dynamic-update-slice_fusion.10
  31.3 1.4 constant_dynamic-update-slice_fusion.9
  32.7 1.4 constant_dynamic-update-slice_fusion.8
  34.2 1.4 constant_dynamic-update-slice_fusion.7
  35.6 1.4 constant_dynamic-update-slice_fusion.6
  37.0 1.4 constant_dynamic-update-slice_fusion.5
  38.4 1.4 constant_dynamic-update-slice_fusion.4
  42.7 1.4 constant_dynamic-update-slice_fusion.1
  45.5 7.1 %all-to-all-start = ((bf16[32,12,8,256]{3,2,1,0:T(8,128)(2,1)}), bf16[32,12,8,256]{3,2,1,0:T(8,128)(2,1)S(1)}, u32[]{:S(2)}, u32[]{:S(2)}) async-start(bf16[32,12,8,256]{3,2,1,0:T(8,128)(2,1)} %constant_dynamic-update-slice_fusion), calls=%async_computation | async-start | bytes 3145728 | tf_op jit(solution)/shard_map/all_to_all | solution.py:48
  52.9 37.1 %all-to-all-done = bf16[32,12,8,256]{3,2,1,0:T(8,128)(2,1)S(1)} async-done(((bf16[32,12,8,256]{3,2,1,0:T(8,128)(2,1)}), bf16[32,12,8,256]{3,2,1,0:T(8,128)(2,1)S(1)}, u32[]{:S(2)}, u32[]{:S(2)}) %all-to-all-start) | async-done | bytes 1572896 | tf_op jit(solution)/shard_map/all_to_all | solution.py:48
  91.8 1.7 fusion.19
  94.6 1.7 convolution_convert_fusion.1
  96.3 7.9 %reshape.160 = bf16[384,8,8,32]{3,2,1,0:T(8,128)(2,1)} reshape(bf16[3072,256]{1,0:T(8,128)(2,1)} %convolution_convert_fusion.1) | data formatting | bytes 3145728 | tf_op jit(solution)/shard_map/reshape | solution.py:63
  104.2 3.1 %convolution_convert_fusion = bf16[3072,256]{1,0:T(8,128)(2,1)} fusion(bf16[3072,256]{1,0:T(8,128)(2,1)} %copy-done.1, bf16[256,256]{1,0:T(8,128)(2,1)S(1)} %copy-done.3), kind=kOutput, calls=%fused_computation.18 | convolution fusion | flops 403439616 | bytes 3276800 | tf_op jit(solution)/shard_map/dot_general | solution.py:62
  107.4 7.9 %reshape.161 = bf16[384,8,8,32]{3,2,1,0:T(8,128)(2,1)} reshape(bf16[3072,256]{1,0:T(8,128)(2,1)} %convolution_convert_fusion) | data formatting | bytes 3145728 | tf_op jit(solution)/shard_map/reshape | solution.py:63
  115.2 3.1 %convolution_convert_fusion.2 = bf16[3072,256]{1,0:T(8,128)(2,1)} fusion(bf16[3072,256]{1,0:T(8,128)(2,1)} %copy-done.1, bf16[256,256]{1,0:T(8,128)(2,1)S(1)} %copy-done.4), kind=kOutput, calls=%fused_computation.20 | convolution fusion | flops 403439616 | bytes 3276800 | tf_op jit(solution)/shard_map/dot_general | solution.py:62
  118.4 7.9 %reshape.159 = bf16[384,8,8,32]{3,2,1,0:T(8,128)(2,1)} reshape(bf16[3072,256]{1,0:T(8,128)(2,1)} %convolution_convert_fusion.2) | data formatting | bytes 3145728 | tf_op jit(solution)/shard_map/reshape | solution.py:63
  126.2 22.9 %fusion.7 = f32[8,8,384,384]{2,3,1,0:T(8,128)} fusion(bf16[384,8,8,32]{3,2,1,0:T(8,128)(2,1)} %reshape.161, bf16[384,8,8,32]{3,2,1,0:T(8,128)(2,1)} %reshape.160), kind=kOutput, calls=%fused_computation.11 | convolution fusion | flops 603979776 | bytes 40894464 | tf_op jit(solution)/shard_map/while/body/eval_jaxpr/qphe,kphe->phqk/dot_general | solution.py:74
  149.2 42.9 %fusion.30 = (f32[8,8,384]{2,1,0:T(8,128)S(1)}, f32[8,8,384,384]{2,3,1,0:T(8,128)}) fusion(f32[8,8,384,384]{2,3,1,0:T(8,128)} %fusion.7, pred[384,384]{0,1:T(8,128)(4,1)S(1)} %compare_and_fusion), kind=kOutput, calls=%fused_computation.85 | output fusion | flops 56623488 | bytes 75743232 | tf_op jit(solution)/shard_map/while/body/eval_jaxpr/sub | solution.py:80
  192.1 18.5 %select_bitcast_fusion = bf16[384,8,8,32]{0,3,2,1:T(8,128)(2,1)} fusion(pred[384]{0:T(512)(128)(4,1)S(1)} %broadcast_compare_fusion, f32[8,8,384,384]{2,3,1,0:T(8,128)} %get-tuple-element.16, f32[8,8,384]{2,1,0:T(8,128)S(1)} %get-tuple-element.15, bf16[384,8,8,32]{3,2,1,0:T(8,128)(2,1)} %reshape.159), kind=kOutput, calls=%fused_computation.36 | convolution fusion | flops 624427008 | bytes 40993152 | tf_op jit(solution)/shard_map/while/body/eval_jaxpr/phqk,kphe->qphe/dot_general | solution.py:83
  210.6 9.9 %copy.27 = bf16[384,8,8,32]{3,2,1,0:T(8,128)(2,1)} copy(bf16[384,8,8,32]{0,3,2,1:T(8,128)(2,1)} %select_bitcast_fusion) | data formatting | bytes 3145728 | tf_op jit(solution)/shard_map/while/body/eval_jaxpr/jit(_where)/select_n | solution.py:86
  220.6 8.4 %reshape.162 = bf16[3072,256]{1,0:T(8,128)(2,1)} reshape(bf16[384,8,8,32]{3,2,1,0:T(8,128)(2,1)} %copy.27) | data formatting | bytes 3145728 | tf_op jit(solution)/shard_map/reshape | solution.py:89
  229.0 2.0 fusion.23
  231.0 40.7 %all_to_all.14 = bf16[384,8,256]{2,1,0:T(8,128)(2,1)S(1)} all-to-all(bf16[384,8,256]{2,1,0:T(8,128)(2,1)S(1)} %fusion.23), channel_id=1, replica_groups=mesh['group'=8,'pos'=4] {'group','pos'}, dimensions={0} | all-to-all | bytes 3145728 | tf_op jit(solution)/shard_map/all_to_all | solution.py:94
  272.2 2.0 copy.28
  275.4 3.1 %fusion.14 = bf16[3072,256]{1,0:T(8,128)(2,1)S(1)} fusion(f32[32,12,8,256]{3,2,0,1:T(8,128)} %copy.28, f32[256]{0:T(256)S(1)} %copy-done.7, f32[3072]{0:T(1024)S(1)} %rsqrt.25, f32[3072]{0:T(1024)S(1)} %div.34), kind=kLoop, calls=%fused_computation.24 | loop fusion | flops 3145728 | bytes 4744192 | tf_op jit(solution)/shard_map/convert_element_type | solution.py:24
  278.6 6.6 %fusion.10 = bf16[3072,256]{1,0:T(8,128)(2,1)} fusion(f32[3072,256]{1,0:T(8,128)} %bitcast.113, bf16[1024,256]{1,0:T(8,128)(2,1)S(1)} %copy-done, bf16[3072,256]{1,0:T(8,128)(2,1)S(1)} %fusion.14, bf16[256,1024]{1,0:T(8,128)(2,1)S(1)} %copy-done.9), kind=kOutput, calls=%fused_computation.16 | convolution fusion | flops 3229089792 | bytes 7340032 | tf_op jit(solution)/shard_map/dot_general | solution.py:33
  (43 shorter events, 9.2 us)
Async XLA Ops:
  0.0 278.6 %copy-start = (bf16[1024,256]{1,0:T(8,128)(2,1)S(1)}, bf16[1024,256]{1,0:T(8,128)(2,1)}, u32[]{:S(2)}) copy-start(bf16[1024,256]{1,0:T(8,128)(2,1)} %param.19) | copy-start | bytes 1572868
  45.5 7.1 %copy-start.8 = (s32[6]{0:T(128)S(1)}, s32[6]{0:T(128)}, u32[]{:S(2)}) copy-start(s32[6]{0:T(128)} %param.21) | copy-start | bytes 76
  45.5 7.1 %copy-start.10 = (s32[6]{0:T(128)S(1)}, s32[6]{0:T(128)}, u32[]{:S(2)}) copy-start(s32[6]{0:T(128)} %param.20) | copy-start | bytes 76
  45.5 44.5 %all-to-all-start = ((bf16[32,12,8,256]{3,2,1,0:T(8,128)(2,1)}), bf16[32,12,8,256]{3,2,1,0:T(8,128)(2,1)S(1)}, u32[]{:S(2)}, u32[]{:S(2)}) async-start(bf16[32,12,8,256]{3,2,1,0:T(8,128)(2,1)} %constant_dynamic-update-slice_fusion), calls=%async_computation | async-start | bytes 3145728 | tf_op jit(solution)/shard_map/all_to_all | solution.py:48
  90.5 1.2 copy-start.6
  91.8 2.8 copy-start.2
  93.5 1.1 copy-start.1
  96.3 7.9 %copy-start.3 = (bf16[256,256]{1,0:T(8,128)(2,1)S(1)}, bf16[256,256]{1,0:T(8,128)(2,1)}, u32[]{:S(2)}) copy-start(bf16[256,256]{1,0:T(8,128)(2,1)} %param.14) | copy-start | bytes 393220
  107.4 7.9 %copy-start.4 = (bf16[256,256]{1,0:T(8,128)(2,1)S(1)}, bf16[256,256]{1,0:T(8,128)(2,1)}, u32[]{:S(2)}) copy-start(bf16[256,256]{1,0:T(8,128)(2,1)} %param.15) | copy-start | bytes 393220
  220.6 8.4 %copy-start.5 = (bf16[256,256]{1,0:T(8,128)(2,1)S(1)}, bf16[256,256]{1,0:T(8,128)(2,1)}, u32[]{:S(2)}) copy-start(bf16[256,256]{1,0:T(8,128)(2,1)} %param.16) | copy-start | bytes 393220
  274.1 1.3 copy-start.7
  275.4 3.2 %copy-start.9 = (bf16[256,1024]{1,0:T(8,128)(2,1)S(1)}, bf16[256,1024]{1,0:T(8,128)(2,1)}, u32[]{:S(2)}) copy-start(bf16[256,1024]{1,0:T(8,128)(2,1)} %param.18) | copy-start | bytes 1572868
